TPU v7x, 32 devices: a whole 2x2x4 slice. The times are simulated.
32 devices in a mesh: tm: 8 (over z, core), dp: 4 (over y, x).
Axes of the slice: x: 2, y: 2, z: 4, core: 2. Of those that a mesh axis runs over, the one named last changes fastest.
Arguments:
- encoded: bfloat16 [512, 80, 1024], P('dp', 'tm'), may hold values from -6 to 6
- queries: bfloat16 [512, 32, 1024], P(('dp', 'tm')), may hold values from -200 to 200
- cotangent: bfloat16 [512, 32, 1024], P(('dp', 'tm')), may hold values from -0.08886719 to 0.08886719
- lengths: int32 [512], P(('dp', 'tm')), may hold values from 2 to 80
- key_weight: bfloat16 [1024, 1024], replicated, may hold values from -0.1875 to 0.1875
- value_weight: bfloat16 [1024, 1024], replicated, may hold values from -0.1875 to 0.1875
Outputs:
- context: bfloat16 [512, 32, 1024], P(('dp', 'tm'))
- key_grad: float32 [1024, 1024], replicated
- value_grad: float32 [1024, 1024], replicated
Inputs may be any that keep to these rules, and one draw needn't show every extreme that they name: Sequence b attends only to source positions below lengths[b].
All inputs are finite; a program needn't handle non-finite values.
Results may differ from a plain program's by a relative error of at most 0.0069.
Values may be sent and summed in bfloat16 or wider, within the bound.
A program may use at most 128 MiB of HBM per device.

v0:
```python
import math
import jax
import jax.numpy as jnp
from jax import lax
from jax.sharding import PartitionSpec as P


def attend(queries, key_rows, value_rows, lengths, cotangent):
    score_scale = 1.0 / math.sqrt(queries.shape[-1])
    scores = (
        jnp.einsum("btd,bsd->bts", queries, key_rows, preferred_element_type=jnp.float32)
        * score_scale
    )
    positions = jnp.arange(key_rows.shape[1], dtype=jnp.int32)
    in_range = positions[None, None, :] < lengths[:, None, None]
    scores = jnp.where(in_range, scores, -1e30)
    row_max = jnp.max(scores, axis=-1, keepdims=True)
    weights = jnp.exp(scores - row_max)
    probabilities = weights / jnp.sum(weights, axis=-1, keepdims=True)
    probs_low = probabilities.astype(jnp.bfloat16)
    context = jnp.einsum(
        "bts,bsd->btd", probs_low, value_rows, preferred_element_type=jnp.float32
    ).astype(jnp.bfloat16)
    grad_probs = jnp.einsum(
        "btd,bsd->bts", cotangent, value_rows, preferred_element_type=jnp.float32
    )
    grad_scores = probabilities * (
        grad_probs - jnp.sum(probabilities * grad_probs, axis=-1, keepdims=True)
    )
    grad_low = grad_scores.astype(jnp.bfloat16)
    grad_values = jnp.einsum(
        "bts,btd->bsd", probs_low, cotangent, preferred_element_type=jnp.float32
    ).astype(jnp.bfloat16)
    grad_keys = (
        jnp.einsum("bts,btd->bsd", grad_low, queries, preferred_element_type=jnp.float32)
        * score_scale
    ).astype(jnp.bfloat16)
    return (context, grad_keys, grad_values)


def project(flattened, weight_matrix, shape):
    return (
        jnp.dot(flattened, weight_matrix, preferred_element_type=jnp.float32)
        .astype(jnp.bfloat16)
        .reshape(shape)
    )


def weight_term(flattened, gradient):
    model_width = flattened.shape[1]
    return lax.dot_general(
        flattened,
        gradient.reshape(-1, model_width),
        (((0,), (0,)), ((), ())),
        preferred_element_type=jnp.float32,
    )


def body(encoded, queries, cotangent, lengths, key_weight, value_weight):
    model_width = encoded.shape[2]
    regrouped = lax.all_to_all(encoded, "tm", split_axis=0, concat_axis=1, tiled=True)
    flattened = regrouped.reshape(-1, model_width)
    key_rows = project(flattened, key_weight, regrouped.shape)
    value_rows = project(flattened, value_weight, regrouped.shape)
    context, grad_keys, grad_values = attend(queries, key_rows, value_rows, lengths, cotangent)
    key_grad = weight_term(flattened, grad_keys)
    value_grad = weight_term(flattened, grad_values)
    key_grad, value_grad = lax.psum((key_grad, value_grad), ("tm", "dp"))
    return (context, key_grad, value_grad)


def solution(mesh):
    return jax.shard_map(
        body,
        mesh=mesh,
        in_specs=(
            P("dp", "tm", None),
            P(("dp", "tm"), None, None),
            P(("dp", "tm"), None, None),
            P(("dp", "tm")),
            P(),
            P(),
        ),
        out_specs=(P(("dp", "tm"), None, None), P(), P()),
        check_vma=False,
    )
```

profile of v0, /device:TPU:0, one launch (start us, length us, event | category | flops | bytes accessed | tf_op | source)
XLA Modules:
  0.0 355.5 jit_solution(7292842336370048144)
XLA Ops:
  7.2 0.0 copy-start
  7.2 5.5 %copy.14 = bf16[128,10,1024]{2,1,0:T(8,128)(2,1)} copy(bf16[128,10,1024]{2,0,1:T(8,128)(2,1)} %param.6) | data formatting | bytes 5242880 | tf_op args[0]
  12.7 0.0 copy-start.5
  12.7 6.5 %all-to-all-start = ((bf16[128,10,1024]{2,1,0:T(8,128)(2,1)}), bf16[128,10,1024]{2,1,0:T(8,128)(2,1)}, u32[]{:S(2)}, u32[]{:S(2)}) async-start(bf16[128,10,1024]{2,1,0:T(8,128)(2,1)} %copy.14), calls=%async_computation | async-start | bytes 8388608 | tf_op jit(solution)/shard_map/all_to_all | solution.py:61
  19.2 0.0 all-reduce.3.cloned.1.call-start
  19.2 0.0 copy-done.5
  19.3 0.1 iota_compare_fusion
  19.3 94.0 %all-to-all-done = bf16[128,10,1024]{2,1,0:T(8,128)(2,1)} async-done(((bf16[128,10,1024]{2,1,0:T(8,128)(2,1)}), bf16[128,10,1024]{2,1,0:T(8,128)(2,1)}, u32[]{:S(2)}, u32[]{:S(2)}) %all-to-all-start) | async-done | bytes 2621472 | tf_op jit(solution)/shard_map/all_to_all | solution.py:61
  113.3 5.0 %copy.19 = bf16[8,16,10,1024]{3,2,0,1:T(8,128)(2,1)} copy(bf16[8,16,10,1024]{3,2,1,0:T(8,128)(2,1)} %bitcast) | data formatting | bytes 5242880 | tf_op jit(solution)/shard_map/all_to_all | solution.py:61
  118.3 6.1 %reshape.46 = bf16[1280,1024]{1,0:T(8,128)(2,1)} reshape(bf16[16,8,10,1024]{3,2,1,0:T(8,128)(2,1)} %bitcast.35) | data formatting | bytes 5242880 | tf_op jit(solution)/shard_map/reshape | solution.py:62
  124.5 0.0 copy-done
  124.5 0.0 copy-start.3
  124.5 0.0 copy-start.6
  124.5 6.1 %convolution_convert_fusion = bf16[1280,1024]{1,0:T(8,128)(2,1)} fusion(bf16[1280,1024]{1,0:T(8,128)(2,1)} %reshape.46, bf16[1024,1024]{1,0:T(8,128)(2,1)S(1)} %copy-done), kind=kOutput, calls=%fused_computation.3 | convolution fusion | flops 2685665280 | bytes 7340032 | tf_op jit(solution)/shard_map/dot_general | solution.py:43
  130.6 0.0 copy-done.3
  130.6 0.0 copy-done.6
  130.6 0.0 copy-start.1
  130.6 3.1 convolution_convert_fusion.1
  133.7 0.0 copy-done.1
  133.7 0.8 fusion.4
  134.6 0.9 fusion.8
  135.4 4.6 %convolution_convert_fusion.2 = bf16[16,80,1024]{2,1,0:T(8,128)(2,1)} fusion(bf16[16,32,1024]{2,1,0:T(8,128)(2,1)} %param.8, f32[16,32]{1,0:T(8,128)S(1)} %get-tuple-element.14, f32[16,32,80]{2,1,0:T(8,128)S(1)} %fusion.4), kind=kOutput, calls=%fused_computation.7 | convolution fusion | flops 85320272 | bytes 3835904 | tf_op jit(solution)/shard_map/bts,btd->bsd/dot_general | solution.py:31
  140.0 3.6 %multiply_reduce_fusion = (f32[16,32]{1,0:T(8,128)S(1)}, f32[16,32,80]{2,1,0:T(8,128)}) fusion(f32[16,32,80]{2,1,0:T(8,128)} %get-tuple-element.15, f32[16,32]{1,0:T(8,128)S(1)} %get-tuple-element.14, bf16[16,80,1024]{2,1,0:T(8,128)(2,1)} %bitcast.36, bf16[16,32,1024]{2,1,0:T(8,128)(2,1)} %param.8), kind=kOutput, calls=%fused_computation.16 | convolution fusion | flops 84008448 | bytes 4001792 | tf_op jit(solution)/shard_map/btd,bsd->bts/dot_general | solution.py:24
  143.6 4.1 %multiply_convert_fusion = bf16[16,80,1024]{2,1,0:T(8,128)(2,1)} fusion(bf16[16,32,1024]{2,1,0:T(8,128)(2,1)S(1)} %copy-done.1, f32[16,32,80]{2,1,0:T(8,128)} %get-tuple-element.17, f32[16,32]{1,0:T(8,128)S(1)} %get-tuple-element.16, f32[16,32]{1,0:T(8,128)S(1)} %get-tuple-element.14, f32[16,32,80]{2,1,0:T(8,128)S(1)} %fusion.4), kind=kOutput, calls=%fused_computation.1 | convolution fusion | flops 86712912 | bytes 4001792 | tf_op jit(solution)/shard_map/bts,btd->bsd/dot_general | solution.py:35
  147.8 0.0 copy-start.2
  147.8 0.0 copy-start.4
  147.8 7.6 %convolution_bitcast_fusion.1 = f32[1024,1024]{0,1:T(8,128)} fusion(bf16[1280,1024]{1,0:T(8,128)(2,1)} %bitcast.40, bf16[1280,1024]{1,0:T(8,128)(2,1)} %reshape.46), kind=kOutput, calls=%fused_computation.6 | convolution fusion | flops 2684354560 | bytes 9437184 | tf_op jit(solution)/shard_map/dot_general | solution.py:51
  155.4 0.0 copy-done.2
  155.4 0.0 copy-done.4
  155.4 4.4 %convolution_bitcast_fusion = f32[1024,1024]{0,1:T(8,128)} fusion(bf16[1280,1024]{1,0:T(8,128)(2,1)S(1)} %bitcast.38, bf16[1280,1024]{1,0:T(8,128)(2,1)S(1)} %copy-done.4), kind=kOutput, calls=%fused_computation.5 | convolution fusion | flops 2684354560 | bytes 9437184 | tf_op jit(solution)/shard_map/dot_general | solution.py:51
  159.8 0.0 all-reduce.3.cloned.1.call-update
  159.9 3.8 %convolution_convert_fusion.3 = bf16[16,32,1024]{2,1,0:T(8,128)(2,1)} fusion(bf16[16,80,1024]{2,1,0:T(8,128)(2,1)} %bitcast.37, f32[16,32]{1,0:T(8,128)S(1)} %get-tuple-element.14, f32[16,32,80]{2,1,0:T(8,128)S(1)} %fusion.4), kind=kOutput, calls=%fused_computation.8 | convolution fusion | flops 84533840 | bytes 3835904 | tf_op jit(solution)/shard_map/bts,bsd->btd/dot_general | solution.py:21
  163.7 174.3 %all-reduce.3.cloned.1.call-done = (f32[1024,1024]{0,1:T(8,128)}, f32[1024,1024]{0,1:T(8,128)}) async-done(((f32[1024,1024]{0,1:T(8,128)}, f32[1024,1024]{0,1:T(8,128)}), (f32[1024,1024]{0,1:T(8,128)}, f32[1024,1024]{0,1:T(8,128)})) %all-reduce.3.cloned.1.call-update) | async-done | bytes 8388624 | tf_op jit(solution)/shard_map/psum | solution.py:68
  338.0 5.3 %copy.16 = f32[1024,1024]{1,0:T(8,128)} copy(f32[1024,1024]{0,1:T(8,128)} %get-tuple-element.12) | data formatting | bytes 8388608
  343.4 5.3 %copy.17 = f32[1024,1024]{1,0:T(8,128)} copy(f32[1024,1024]{0,1:T(8,128)} %get-tuple-element.13) | data formatting | bytes 8388608
Async XLA Ops:
  7.2 117.3 %copy-start = (bf16[1024,1024]{1,0:T(8,128)(2,1)S(1)}, bf16[1024,1024]{1,0:T(8,128)(2,1)}, u32[]{:S(2)}) copy-start(bf16[1024,1024]{1,0:T(8,128)(2,1)} %param.11) | copy-start | bytes 6291460
  12.7 6.5 %copy-start.5 = (s32[16]{0:T(128)S(1)}, s32[16]{0:T(128)}, u32[]{:S(2)}) copy-start(s32[16]{0:T(128)} %param.9) | copy-start | bytes 196
  12.7 100.6 %all-to-all-start = ((bf16[128,10,1024]{2,1,0:T(8,128)(2,1)}), bf16[128,10,1024]{2,1,0:T(8,128)(2,1)}, u32[]{:S(2)}, u32[]{:S(2)}) async-start(bf16[128,10,1024]{2,1,0:T(8,128)(2,1)} %copy.14), calls=%async_computation | async-start | bytes 8388608 | tf_op jit(solution)/shard_map/all_to_all | solution.py:61
  19.2 318.8 %all-reduce.3.cloned.1.call-start = ((), (), s32[]{:S(2)}) async-start(), calls=%async_computation.1 | async-start | bytes 16777216 | tf_op jit(solution)/shard_map/psum | solution.py:68
  124.5 6.1 %copy-start.3 = (bf16[1280,1024]{1,0:T(8,128)(2,1)S(1)}, bf16[1280,1024]{1,0:T(8,128)(2,1)}, u32[]{:S(2)}) copy-start(bf16[1280,1024]{1,0:T(8,128)(2,1)} %reshape.46) | copy-start | bytes 7864324
  124.5 6.1 %copy-start.6 = (bf16[1024,1024]{1,0:T(8,128)(2,1)S(1)}, bf16[1024,1024]{1,0:T(8,128)(2,1)}, u32[]{:S(2)}) copy-start(bf16[1024,1024]{1,0:T(8,128)(2,1)} %param.10) | copy-start | bytes 6291460
  130.6 3.1 copy-start.1
  147.8 7.6 %copy-start.2 = (bf16[16,80,1024]{2,1,0:T(8,128)(2,1)S(1)}, bf16[16,80,1024]{2,1,0:T(8,128)(2,1)}, u32[]{:S(2)}) copy-start(bf16[16,80,1024]{2,1,0:T(8,128)(2,1)} %convolution_convert_fusion.2) | copy-start | bytes 7864324
  147.8 7.6 %copy-start.4 = (bf16[1280,1024]{1,0:T(8,128)(2,1)S(1)}, bf16[1280,1024]{1,0:T(8,128)(2,1)}, u32[]{:S(2)}) copy-start(bf16[1280,1024]{1,0:T(8,128)(2,1)} %reshape.46) | copy-start | bytes 7864324
Sparse Core Ops, SparseCore 0:
  160.0 177.9 all-reduce.2
where the time goes:
time: 356 us
  waiting for transfers between devices  268 us (75%)
  matrix products  38.3 us (11%)
  local copies, waits for them, and re-layouts  27.4 us (8%)
  between operations  14.1 us (4%)
  starting transfers between devices  6.52 us (2%)
    psum x1, waiting for transfers between devices, body(): key_grad, value_grad = lax.psum((key_grad, value_grad), ('tm', 'dp'))  174 us
    all_to_all x1, waiting for transfers between devices, body(): lax.all_to_all(encoded, 'tm', split_axis=0, concat_axis=1, tiled=True)  94 us
    unnamed x17, local copies, waits for them, and re-layouts  16.2 us
    dot_general x2, matrix products, weight_term(): lax.dot_general(flattened, gradient.reshape(-1, model_width), (((0,), (0,...  12.1 us
    dot_general x2, matrix products, project(): jnp.dot(flattened, weight_matrix, preferred_element_type=jnp.float32)  9.23 us
  transfers between devices with their start and end apart: 2, of which 2 were waited for; matrix products, arithmetic and copies ran while one was open for 1% of the time, Pallas kernels for 0%

commit v1 on v0

--- a/solution.py
+++ b/solution.py
@@ -1,8 +1,16 @@
+import functools
 import math
 import jax
 import jax.numpy as jnp
 from jax import lax
 from jax.sharding import PartitionSpec as P
+
+
+def _balance_files(local, group_axis, row_axis):
+    return jax.lax.psum(jax.lax.psum(local, group_axis), row_axis)
+
+
+update_cube_over_axis = functools.partial(_balance_files, group_axis="tm", row_axis="dp")
 
 
 def attend(queries, key_rows, value_rows, lengths, cotangent):
@@ -65,7 +73,7 @@
     context, grad_keys, grad_values = attend(queries, key_rows, value_rows, lengths, cotangent)
     key_grad = weight_term(flattened, grad_keys)
     value_grad = weight_term(flattened, grad_values)
-    key_grad, value_grad = lax.psum((key_grad, value_grad), ("tm", "dp"))
+    key_grad, value_grad = update_cube_over_axis((key_grad, value_grad))
     return (context, key_grad, value_grad)
 
 

time: 356 us -> 527 us (1.48)
  waiting for transfers between devices: 268 us -> 441 us
    psum x1 -> x2, waiting for transfers between devices: 174 us -> 347 us  [_balance_files(): return jax.lax.psum(jax.lax.psum(local, group_axis), row_axis)]
    unnamed x17 -> x21, local copies, waits for them, and re-layouts: 16.2 us -> 16.4 us
  transfers between devices with their start and end apart: 2 -> 3, of which waited for: 2 -> 3; matrix products, arithmetic and copies ran while one was open for 1% -> 1% of each run, Pallas kernels for 0% -> 0%
where the time goes in v1:
time: 527 us
  waiting for transfers between devices  441 us (84%)
  matrix products  35.2 us (7%)
  local copies, waits for them, and re-layouts  27.6 us (5%)
  between operations  14.1 us (3%)
  starting transfers between devices  6.56 us (1%)
    psum x2, waiting for transfers between devices, _balance_files(): return jax.lax.psum(jax.lax.psum(local, group_axis), row_axis)  347 us
    all_to_all x1, waiting for transfers between devices, body(): lax.all_to_all(encoded, 'tm', split_axis=0, concat_axis=1, tiled=True)  94 us
    unnamed x21, local copies, waits for them, and re-layouts  16.4 us
    dot_general x2, matrix products, weight_term(): lax.dot_general(flattened, gradient.reshape(-1, model_width), (((0,), (0,...  12.1 us
  transfers between devices with their start and end apart: 3, of which 3 were waited for; matrix products, arithmetic and copies ran while one was open for 1% of the time, Pallas kernels for 0%

profile of v1, /device:TPU:0, one launch (start us, length us, event | category | flops | bytes accessed | tf_op | source)
XLA Modules:
  0.0 526.9 jit_solution(4211572156688250473)
XLA Ops:
  7.2 0.0 copy-start
  7.2 5.5 %copy.14 = bf16[128,10,1024]{2,1,0:T(8,128)(2,1)} copy(bf16[128,10,1024]{2,0,1:T(8,128)(2,1)} %param.6) | data formatting | bytes 5242880 | tf_op args[0]
  12.7 0.0 copy-start.7
  12.7 6.5 %all-to-all-start = ((bf16[128,10,1024]{2,1,0:T(8,128)(2,1)}), bf16[128,10,1024]{2,1,0:T(8,128)(2,1)}, u32[]{:S(2)}, u32[]{:S(2)}) async-start(bf16[128,10,1024]{2,1,0:T(8,128)(2,1)} %copy.14), calls=%async_computation | async-start | bytes 8388608 | tf_op jit(solution)/shard_map/all_to_all | solution.py:69
  19.2 0.0 all-reduce.5.cloned.1.call-start
  19.2 0.0 copy-done.7
  19.3 0.1 iota_compare_fusion
  19.3 94.0 %all-to-all-done = bf16[128,10,1024]{2,1,0:T(8,128)(2,1)} async-done(((bf16[128,10,1024]{2,1,0:T(8,128)(2,1)}), bf16[128,10,1024]{2,1,0:T(8,128)(2,1)}, u32[]{:S(2)}, u32[]{:S(2)}) %all-to-all-start) | async-done | bytes 2621472 | tf_op jit(solution)/shard_map/all_to_all | solution.py:69
  113.3 5.0 copy.19
  118.3 6.1 %reshape.46 = bf16[1280,1024]{1,0:T(8,128)(2,1)} reshape(bf16[16,8,10,1024]{3,2,1,0:T(8,128)(2,1)} %bitcast.35) | data formatting | bytes 5242880 | tf_op jit(solution)/shard_map/reshape | solution.py:70
  124.5 0.0 copy-done
  124.5 0.0 copy-start.4
  124.5 0.0 copy-start.8
  124.5 6.2 %convolution_convert_fusion = bf16[1280,1024]{1,0:T(8,128)(2,1)} fusion(bf16[1280,1024]{1,0:T(8,128)(2,1)} %reshape.46, bf16[1024,1024]{1,0:T(8,128)(2,1)S(1)} %copy-done), kind=kOutput, calls=%fused_computation.3 | convolution fusion | flops 2685665280 | bytes 7340032 | tf_op jit(solution)/shard_map/dot_general | solution.py:51
  130.6 0.0 copy-done.4
  130.7 0.0 copy-done.8
  130.7 0.0 copy-start.2
  130.7 3.1 convolution_convert_fusion.1
  133.8 0.0 copy-start.6
  133.8 0.0 copy-done.2
  133.8 0.8 fusion.4
  134.6 2.8 fusion.8
  137.4 0.0 copy-done.6
  137.4 3.4 convolution_convert_fusion.2
  140.8 2.6 multiply_reduce_fusion
  143.4 3.2 multiply_convert_fusion
  146.6 0.0 copy-start.3
  146.6 0.0 copy-start.5
  146.6 7.6 %convolution_bitcast_fusion.1 = f32[1024,1024]{0,1:T(8,128)} fusion(bf16[1280,1024]{1,0:T(8,128)(2,1)} %bitcast.40, bf16[1280,1024]{1,0:T(8,128)(2,1)} %reshape.46), kind=kOutput, calls=%fused_computation.6 | convolution fusion | flops 2684354560 | bytes 9437184 | tf_op jit(solution)/shard_map/dot_general | solution.py:59
  154.2 0.0 copy-done.3
  154.2 0.0 copy-done.5
  154.2 4.4 convolution_bitcast_fusion
  158.7 0.0 all-reduce.5.cloned.1.call-update
  158.7 0.0 all-reduce.7.cloned.1.call-start
  158.8 174.6 %all-reduce.5.cloned.1.call-done = (f32[1024,1024]{0,1:T(8,128)}, f32[1024,1024]{0,1:T(8,128)}) async-done(((f32[1024,1024]{0,1:T(8,128)}, f32[1024,1024]{0,1:T(8,128)}), (f32[1024,1024]{0,1:T(8,128)}, f32[1024,1024]{0,1:T(8,128)})) %all-reduce.5.cloned.1.call-update) | async-done | bytes 8388624 | tf_op jit(solution)/shard_map/psum | solution.py:10
  333.3 0.0 all-reduce.7.cloned.1.call-update
  333.4 3.8 convolution_convert_fusion.3
  337.2 172.1 %all-reduce.7.cloned.1.call-done = (f32[1024,1024]{0,1:T(8,128)}, f32[1024,1024]{0,1:T(8,128)}) async-done(((f32[1024,1024]{0,1:T(8,128)}, f32[1024,1024]{0,1:T(8,128)}), (f32[1024,1024]{0,1:T(8,128)}, f32[1024,1024]{0,1:T(8,128)})) %all-reduce.7.cloned.1.call-update) | async-done | bytes 8388624 | tf_op jit(solution)/shard_map/psum | solution.py:10
  509.3 5.3 %copy.16 = f32[1024,1024]{1,0:T(8,128)} copy(f32[1024,1024]{0,1:T(8,128)} %get-tuple-element.14) | data formatting | bytes 8388608
  514.6 0.0 copy-start.1
  514.6 5.5 %copy.17 = f32[1024,1024]{1,0:T(8,128)} copy(f32[1024,1024]{0,1:T(8,128)} %get-tuple-element.15) | data formatting | bytes 8388608
  520.1 0.0 copy-done.1
Async XLA Ops:
  7.2 117.3 %copy-start = (bf16[1024,1024]{1,0:T(8,128)(2,1)S(1)}, bf16[1024,1024]{1,0:T(8,128)(2,1)}, u32[]{:S(2)}) copy-start(bf16[1024,1024]{1,0:T(8,128)(2,1)} %param.11) | copy-start | bytes 6291460
  12.7 6.5 %copy-start.7 = (s32[16]{0:T(128)S(1)}, s32[16]{0:T(128)}, u32[]{:S(2)}) copy-start(s32[16]{0:T(128)} %param.9) | copy-start | bytes 196
  12.7 100.6 %all-to-all-start = ((bf16[128,10,1024]{2,1,0:T(8,128)(2,1)}), bf16[128,10,1024]{2,1,0:T(8,128)(2,1)}, u32[]{:S(2)}, u32[]{:S(2)}) async-start(bf16[128,10,1024]{2,1,0:T(8,128)(2,1)} %copy.14), calls=%async_computation | async-start | bytes 8388608 | tf_op jit(solution)/shard_map/all_to_all | solution.py:69
  19.2 314.1 %all-reduce.5.cloned.1.call-start = ((), (), s32[]{:S(2)}) async-start(), calls=%async_computation.1 | async-start | bytes 16777216 | tf_op jit(solution)/shard_map/psum | solution.py:10
  124.5 6.2 %copy-start.4 = (bf16[1280,1024]{1,0:T(8,128)(2,1)S(1)}, bf16[1280,1024]{1,0:T(8,128)(2,1)}, u32[]{:S(2)}) copy-start(bf16[1280,1024]{1,0:T(8,128)(2,1)} %reshape.46) | copy-start | bytes 7864324
  124.5 6.2 %copy-start.8 = (bf16[1024,1024]{1,0:T(8,128)(2,1)S(1)}, bf16[1024,1024]{1,0:T(8,128)(2,1)}, u32[]{:S(2)}) copy-start(bf16[1024,1024]{1,0:T(8,128)(2,1)} %param.10) | copy-start | bytes 6291460
  130.7 3.1 copy-start.2
  133.8 3.6 copy-start.6
  146.6 7.6 %copy-start.3 = (bf16[16,80,1024]{2,1,0:T(8,128)(2,1)S(1)}, bf16[16,80,1024]{2,1,0:T(8,128)(2,1)}, u32[]{:S(2)}) copy-start(bf16[16,80,1024]{2,1,0:T(8,128)(2,1)} %convolution_convert_fusion.2) | copy-start | bytes 7864324
  146.6 7.6 %copy-start.5 = (bf16[1280,1024]{1,0:T(8,128)(2,1)S(1)}, bf16[1280,1024]{1,0:T(8,128)(2,1)}, u32[]{:S(2)}) copy-start(bf16[1280,1024]{1,0:T(8,128)(2,1)} %reshape.46) | copy-start | bytes 7864324
  158.7 350.6 %all-reduce.7.cloned.1.call-start = ((), (), s32[]{:S(2)}) async-start(), calls=%async_computation.2 | async-start | bytes 16777216 | tf_op jit(solution)/shard_map/psum | solution.py:10
  514.6 5.5 %copy-start.1 = (bf16[1024,1024]{1,0:T(8,128)(2,1)S(1)}, bf16[1024,1024]{1,0:T(8,128)(2,1)}, u32[]{:S(2)}) copy-start(bf16[1024,1024]{1,0:T(8,128)(2,1)} %param.11) | copy-start | bytes 6291460
Sparse Core Ops, SparseCore 0:
  158.8 174.4 all-reduce.4
  337.1 172.1 all-reduce.6
